TPU v7x, 32 devices: a whole 2x2x4 slice. The times are simulated.
32 devices in a mesh: gx: 4 (over x, core), gy: 4 (over z), gz: 2 (over y).
Axes of the slice: x: 2, y: 2, z: 4, core: 2. Of those that a mesh axis runs over, the one named last changes fastest.
Arguments:
- kappa: float32 [5, 5, 5, 4, 4, 128], P(None, None, None, 'gx', 'gy', 'gz'), may hold values from 0.2 to 5
- source: float32 [5, 5, 5, 4, 4, 128], P(None, None, None, 'gx', 'gy', 'gz'), may hold values from -24 to 24
Outputs:
- solution: float32 [16, 16, 512], P('gx', 'gy', 'gz')
- residual: float32 [16, 16, 512], P('gx', 'gy', 'gz')
All inputs are finite; a program needn't handle non-finite values.
Results may differ from a plain program's by a relative error of at most 0.0003.
Values sent between devices are 32-bit elements; how exact they have to be, the bound alone decides.
No kernel may reach another device: no remote copies, remote signals or barrier semaphores. Data moves between devices by JAX's collectives and lax.ppermute only.
A program may use at most 64 MiB of HBM per device.

v0:
```python
import math

import jax
import jax.numpy as jnp
import numpy as np
from jax import lax
from jax.sharding import PartitionSpec as P

LEVELS = 3


relax_weight = 0.6


def extended(cells, sides, width):
    for axis, dim in sides:
        count = lax.axis_size(axis)
        ends = count - 1
        head = lax.slice_in_dim(cells, 0, width, axis=dim)
        tail = lax.slice_in_dim(cells, cells.shape[dim] - width, cells.shape[dim], axis=dim)
        cells = jnp.concatenate(
            [
                lax.ppermute(tail, axis, [(i, (i + 1) % count) for i in range(ends)]),
                cells,
                lax.ppermute(head, axis, [((i + 1) % count, i) for i in range(ends)]),
            ],
            axis=dim,
        )
    return cells


def gll_tables():
    points = np.array([-1.0, -math.sqrt(3.0 / 7.0), 0.0, math.sqrt(3.0 / 7.0), 1.0])
    quad_weights = np.array([0.1, 49.0 / 90.0, 32.0 / 45.0, 49.0 / 90.0, 0.1])
    bary = np.array(
        [np.prod([points[i] - points[k] for k in range(5) if k != i]) for i in range(5)]
    )
    deriv = np.zeros((5, 5))
    for i in range(5):
        for j in range(5):
            if i != j:
                deriv[i, j] = bary[i] / (bary[j] * (points[i] - points[j]))
    for i in range(5):
        deriv[i, i] = -np.sum(deriv[i])
    return (
        jnp.asarray(points, jnp.float32),
        jnp.asarray(quad_weights, jnp.float32),
        jnp.asarray(deriv, jnp.float32),
    )


def split_first(values):
    count = (values.shape[0] - 1) // 4
    lower = jnp.swapaxes(values[:-1].reshape((count, 4) + values.shape[1:]), 0, 1)
    return jnp.concatenate([lower, values[4::4][None]], axis=0)


def merge_first(block):
    count = block.shape[1]
    rest = block.shape[2:]
    lower = jnp.swapaxes(block[:4], 0, 1).reshape((4 * count,) + rest)
    tail = jnp.concatenate([jnp.zeros((count, 3) + rest, block.dtype), block[4][:, None]], axis=1)
    tail = tail.reshape((4 * count,) + rest)
    spare = [(0, 0)] * len(rest)
    return jnp.pad(lower, [(0, 1)] + spare) + jnp.pad(tail, [(1, 0)] + spare)


def element_view(field):
    element_portion = split_first(field)
    element_portion = split_first(jnp.moveaxis(element_portion, 2, 0))
    element_portion = split_first(jnp.moveaxis(element_portion, 4, 0))
    return jnp.transpose(element_portion, (4, 2, 0, 5, 3, 1))


def node_sum(block):
    element_portion = jnp.transpose(block, (2, 5, 1, 4, 0, 3))
    element_portion = jnp.moveaxis(merge_first(element_portion), 0, 4)
    element_portion = jnp.moveaxis(merge_first(element_portion), 0, 2)
    return merge_first(element_portion)


def stiffness_terms(field, weighted, deriv):
    highest = lax.Precision.HIGHEST
    local = element_view(field)
    grad_x = jnp.einsum("ia,abcxyz->ibcxyz", deriv, local, precision=highest)
    grad_y = jnp.einsum("jb,abcxyz->ajcxyz", deriv, local, precision=highest)
    grad_z = jnp.einsum("kc,abcxyz->abkxyz", deriv, local, precision=highest)
    back = jnp.einsum("ia,ibcxyz->abcxyz", deriv, weighted * grad_x, precision=highest)
    back = back + jnp.einsum("jb,ajcxyz->abcxyz", deriv, weighted * grad_y, precision=highest)
    back = back + jnp.einsum("kc,abkxyz->abcxyz", deriv, weighted * grad_z, precision=highest)
    return node_sum(back)


def mass_pair(paired, width):
    return jnp.stack(
        [width / 6.0 * (2.0 * paired[0] + paired[1]), width / 6.0 * (paired[0] + 2.0 * paired[1])]
    )


def stiff_pair(paired, width):
    slope = (paired[0] - paired[1]) / width
    return jnp.stack([slope, -slope])


def lor_terms(field, coeff, spacing):
    width_x, width_y, width_z = spacing
    zpairs = jnp.stack([field[:, :, :-1], field[:, :, 1:]])
    zmass = mass_pair(zpairs, width_z)
    stiffness_along_z = stiff_pair(zpairs, width_z)
    ymass = jnp.stack([zmass[:, :, :-1], zmass[:, :, 1:]])
    ystiff = jnp.stack([stiffness_along_z[:, :, :-1], stiffness_along_z[:, :, 1:]])
    column_y = width_y[:, None]
    first = mass_pair(ymass, column_y)
    second = stiff_pair(ymass, column_y) + mass_pair(ystiff, column_y)
    column_x = width_x[:, None, None]
    xfirst = jnp.stack([first[:, :, :-1], first[:, :, 1:]])
    xsecond = jnp.stack([second[:, :, :-1], second[:, :, 1:]])
    cells = (stiff_pair(xfirst, column_x) + mass_pair(xsecond, column_x)) * coeff
    total = jnp.zeros(field.shape, jnp.float32)
    for a in range(2):
        for b in range(2):
            for c in range(2):
                total = total + jnp.pad(cells[a, b, c], ((a, 1 - a), (b, 1 - b), (c, 1 - c)))
    return total


def lor_diagonal(coeff, spacing):
    width_x = spacing[0][:, None, None]
    width_y = spacing[1][None, :, None]
    width_z = spacing[2][None, None, :]
    cells = coeff * (
        width_y * width_z / (9.0 * width_x)
        + width_x * width_z / (9.0 * width_y)
        + width_x * width_y / (9.0 * width_z)
    )
    shape = tuple((n + 1 for n in coeff.shape))
    total = jnp.zeros(shape, jnp.float32)
    for a in range(2):
        for b in range(2):
            for c in range(2):
                total = total + jnp.pad(cells, ((a, 1 - a), (b, 1 - b), (c, 1 - c)))
    return total


def subcell_coefficient(kappa):
    averaged = 0.5 * (kappa[:-1] + kappa[1:])
    averaged = 0.5 * (averaged[:, :-1] + averaged[:, 1:])
    averaged = 0.5 * (averaged[:, :, :-1] + averaged[:, :, 1:])
    count_x, count_y, count_z = averaged.shape[3:]
    return jnp.transpose(averaged, (3, 0, 4, 1, 5, 2)).reshape(
        4 * count_x, 4 * count_y, 4 * count_z
    )


def coarsen(coeff):
    nx, ny, nz = coeff.shape
    return jnp.mean(coeff.reshape(nx // 2, 2, ny // 2, 2, nz // 2, 2), axis=(1, 3, 5))


def interp_weights(width):
    paired = width.reshape(-1, 2)
    span = paired[:, 0] + paired[:, 1]
    return (paired[:, 1] / span, paired[:, 0] / span)


def prolong_first(coarse, left, right):
    shape = (-1,) + (1,) * (coarse.ndim - 1)
    middle = left.reshape(shape) * coarse[:-1] + right.reshape(shape) * coarse[1:]
    woven = jnp.stack([coarse[:-1], middle], axis=1).reshape(
        (2 * (coarse.shape[0] - 1),) + coarse.shape[1:]
    )
    return jnp.concatenate([woven, coarse[-1:]], axis=0)


def restrict_first(fine, left, right):
    shape = (-1,) + (1,) * (fine.ndim - 1)
    middle = fine[1::2]
    spare = [(0, 0)] * (fine.ndim - 1)
    return (
        fine[0::2]
        + jnp.pad(left.reshape(shape) * middle, [(0, 1)] + spare)
        + jnp.pad(right.reshape(shape) * middle, [(1, 0)] + spare)
    )


def prolong(coarse, weight_sets):
    for axis in range(3):
        left, right = weight_sets[axis]
        coarse = jnp.moveaxis(prolong_first(jnp.moveaxis(coarse, axis, 0), left, right), 0, axis)
    return coarse


def restrict(fine, weight_sets):
    for axis in range(3):
        left, right = weight_sets[axis]
        fine = jnp.moveaxis(restrict_first(jnp.moveaxis(fine, axis, 0), left, right), 0, axis)
    return fine


def collapse_leading(padded):
    inner = padded[1:-1]
    head = inner[0] + padded[0]
    tail = inner[-1] + padded[-1]
    return jnp.concatenate([head[None], inner[1:-1], tail[None]], axis=0)


def fold_axis(padded, axis):
    return jnp.moveaxis(collapse_leading(jnp.moveaxis(padded, axis, 0)), 0, axis)


def assemble(partial_value):
    padded = extended(partial_value, (("gx", 0), ("gy", 1), ("gz", 2)), 1)
    return fold_axis(fold_axis(fold_axis(padded, 0), 1), 2)


def side_mask(cells, position, devices):
    index = position * cells + jnp.arange(cells + 1)
    return ((index > 0) & (index < cells * devices)).astype(jnp.float32)


def block_mask(shape):
    mask_x = side_mask(shape[0], lax.axis_index("gx"), lax.axis_size("gx"))
    mask_y = side_mask(shape[1], lax.axis_index("gy"), lax.axis_size("gy"))
    mask_z = side_mask(shape[2], lax.axis_index("gz"), lax.axis_size("gz"))
    return mask_x[:, None, None] * mask_y[None, :, None] * mask_z[None, None, :]


def owned_mask(shape):
    sides = [(jnp.arange(n + 1) >= 1).astype(jnp.float32) for n in shape]
    return sides[0][:, None, None] * sides[1][None, :, None] * sides[2][None, None, :]


def cycle(level, forcing, levels):
    coeff, spacing, diag, mask, weight_sets, owned = levels[level]
    guess = relax_weight * forcing / diag
    if level == LEVELS - 1:
        guess = (
            guess
            + relax_weight * (forcing - mask * assemble(lor_terms(guess, coeff, spacing))) / diag
        )
        return guess
    defect = forcing * owned - lor_terms(guess, coeff, spacing)
    coarse = levels[level + 1][3] * assemble(restrict(defect, weight_sets))
    guess = guess + prolong(cycle(level + 1, coarse, levels), weight_sets)
    return (
        guess + relax_weight * (forcing - mask * assemble(lor_terms(guess, coeff, spacing))) / diag
    )


def inner_pair(resid, precond, image):
    local_rho = jnp.sum(resid[1:, 1:, 1:] * precond[1:, 1:, 1:])
    local_curv = jnp.sum(precond[1:, 1:, 1:] * image[1:, 1:, 1:])
    return lax.psum((local_rho, local_curv), ("gx", "gy", "gz"))


def body(kappa, source):
    points, quad_weights, deriv = gll_tables()
    cube = (
        quad_weights[:, None, None] * quad_weights[None, :, None] * quad_weights[None, None, :]
    ).reshape(5, 5, 5, 1, 1, 1)
    weighted = kappa * cube
    counts = kappa.shape[3:]
    finest_mask = block_mask([4 * c for c in counts])
    rhs = finest_mask * assemble(node_sum(cube * source))
    gaps = points[1:] - points[:-1]
    spacing = [jnp.tile(gaps, c) for c in counts]
    coeff = subcell_coefficient(kappa)
    levels = []
    for level in range(LEVELS):
        weight_sets = [interp_weights(h) for h in spacing] if level < LEVELS - 1 else None
        diag = assemble(lor_diagonal(coeff, spacing))
        levels.append(
            (coeff, spacing, diag, block_mask(coeff.shape), weight_sets, owned_mask(coeff.shape))
        )
        if level < LEVELS - 1:
            coeff = coarsen(coeff)
            spacing = [h.reshape(-1, 2).sum(axis=1) for h in spacing]

    def operator(field):
        return finest_mask * assemble(stiffness_terms(field, weighted, deriv))

    resid = rhs
    precond = cycle(0, resid, levels)
    image = operator(precond)
    rho_old, curv = inner_pair(resid, precond, image)
    alpha = rho_old / curv
    direction, along = (precond, image)
    iterate = alpha * direction
    resid = resid - alpha * along
    precond = cycle(0, resid, levels)
    image = operator(precond)
    rho_new, curv = inner_pair(resid, precond, image)
    ratio = rho_new / rho_old
    alpha = rho_new / (curv - ratio * rho_new / alpha)
    direction = precond + ratio * direction
    along = image + ratio * along
    iterate = iterate + alpha * direction
    resid = resid - alpha * along
    return (iterate[1:, 1:, 1:], resid[1:, 1:, 1:])


def solution(mesh):
    placed = (P(None, None, None, "gx", "gy", "gz"), P(None, None, None, "gx", "gy", "gz"))
    return jax.shard_map(
        body,
        mesh=mesh,
        in_specs=placed,
        out_specs=(P("gx", "gy", "gz"), P("gx", "gy", "gz")),
        check_vma=False,
    )
```

profile of v0, /device:TPU:0, one launch (start us, length us, event | category | flops | bytes accessed | tf_op | source)
XLA Modules:
  0.0 476.5 jit_solution(2688961487254693226)
XLA Ops:
  3.1 2.4 collective-permute-start.6
  7.3 5.1 %collective-permute-start.18 = (f32[1,3,129]{2,1,0:T(4,128)S(1)}, f32[1,3,129]{2,1,0:T(4,128)S(1)}, u32[]{:S(2)}, u32[]{:S(2)}) collective-permute-start(f32[1,3,129]{2,1,0:T(4,128)S(1)} %get-tuple-element.387), channel_id=1, source_target_pairs={{0,8},{8,16},{16,24},{1,9},{9,17},{17,25},{2,10},{10,18},{18,26},{... | collective-permute-start | bytes 4652 | tf_op jit(solution)/shard_map/ppermute | solution.py:23
  12.8 3.6 collective-permute-start.30
  23.6 3.7 collective-permute-start
  27.3 3.5 collective-permute-start.32
  32.2 4.1 collective-permute-done.33
  36.4 3.4 collective-permute-start.34
  41.2 3.5 collective-permute-start.20
  46.8 4.1 collective-permute-done.21
  50.9 3.8 collective-permute-start.22
  57.5 2.9 collective-permute-done.23
  60.6 3.5 collective-permute-start.8
  65.5 4.5 collective-permute-start.2
  75.6 3.3 collective-permute-start.4
  80.7 4.0 collective-permute-done.5
  91.8 4.1 collective-permute-done.13
  95.9 4.5 collective-permute-start.14
  101.8 4.1 collective-permute-done.15
  109.1 4.2 collective-permute-done.17
  117.3 4.1 collective-permute-done.25
  121.5 1.9 collective-permute-start.26
  124.9 4.0 collective-permute-done.27
  131.9 4.2 collective-permute-done.29
  139.5 4.2 collective-permute-done.37
  143.7 1.9 collective-permute-start.38
  147.0 4.2 collective-permute-done.39
  154.2 4.2 collective-permute-done.41
  162.5 4.2 collective-permute-done.43
  166.6 1.9 collective-permute-start.44
  169.9 4.2 collective-permute-done.45
  177.3 4.2 collective-permute-done.47
  188.7 4.2 collective-permute-done.49
  192.9 1.9 collective-permute-start.50
  196.2 4.2 collective-permute-done.51
  203.7 4.2 collective-permute-done.53
  219.4 3.8 collective-permute-done.55
  226.5 4.2 collective-permute-done.57
  234.0 4.2 collective-permute-done.59
  239.6 38.3 %all-reduce.156 = (f32[]{:T(128)}, f32[]{:T(128)}) all-reduce(f32[]{:T(128)} %get-tuple-element.13, f32[]{:T(128)} %get-tuple-element.12), channel_id=1, replica_groups=mesh['gx'=4,'gy'=4,'gz'=2] {'gx','gy','gz'}, use_global_device_ids=true, to_apply=%region_6.7 | all-reduce | flops 2 | bytes 16 | tf_op jit(solution)/shard_map/psum | solution.py:253
  283.7 4.3 collective-permute-done.61
  288.0 3.8 collective-permute-start.62
  293.2 4.2 collective-permute-done.63
  297.4 4.1 collective-permute-start.64
  303.0 4.2 collective-permute-done.65
  311.2 4.2 collective-permute-done.67
  315.3 2.6 collective-permute-start.68
  319.2 4.2 collective-permute-done.69
  326.4 4.2 collective-permute-done.71
  334.1 4.2 collective-permute-done.73
  338.3 1.9 collective-permute-start.74
  341.5 4.2 collective-permute-done.75
  348.8 4.2 collective-permute-done.77
  357.0 4.2 collective-permute-done.79
  361.2 1.9 collective-permute-start.80
  364.5 4.2 collective-permute-done.81
  371.9 4.1 collective-permute-done.83
  381.9 4.2 collective-permute-done.85
  386.1 1.9 collective-permute-start.86
  389.4 4.2 collective-permute-done.87
  396.9 4.2 collective-permute-done.89
  411.9 3.8 collective-permute-done.91
  419.0 4.2 collective-permute-done.93
  426.5 4.2 collective-permute-done.95
  432.2 38.3 %all-reduce.155 = (f32[]{:T(128)}, f32[]{:T(128)}) all-reduce(f32[]{:T(128)} %get-tuple-element.11, f32[]{:T(128)} %get-tuple-element.10), channel_id=1, replica_groups=mesh['gx'=4,'gy'=4,'gz'=2] {'gx','gy','gz'}, use_global_device_ids=true, to_apply=%region_10.11 | all-reduce | flops 2 | bytes 16 | tf_op jit(solution)/shard_map/psum | solution.py:253
  (714 shorter events, 155.9 us)
Async XLA Ops:
  3.1 57.5 %collective-permute-start.6 = (f32[1,5,257]{2,1,0:T(8,128)S(1)}, f32[1,5,257]{2,1,0:T(8,128)S(1)}, u32[]{:S(2)}, u32[]{:S(2)}) collective-permute-start(f32[1,5,257]{2,1,0:T(8,128)S(1)} %get-tuple-element.233), channel_id=1, source_target_pairs={{0,8},{8,16},{16,24},{1,9},{9,17},{17,25},{2,10},{10,18},{18,26},{... | collective-permute-start | bytes 15428 | tf_op jit(solution)/shard_map/ppermute | solution.py:23
  5.5 55.1 %collective-permute-start.7 = (f32[1,5,257]{2,1,0:T(8,128)S(1)}, f32[1,5,257]{2,1,0:T(8,128)S(1)}, u32[]{:S(2)}, u32[]{:S(2)}) collective-permute-start(f32[1,5,257]{2,1,0:T(8,128)S(1)} %get-tuple-element.234), channel_id=1, source_target_pairs={{8,0},{16,8},{24,16},{9,1},{17,9},{25,17},{10,2},{18,10},{26,18},{... | collective-permute-start | bytes 15428 | tf_op jit(solution)/shard_map/ppermute | solution.py:25
  7.3 20.0 %collective-permute-start.18 = (f32[1,3,129]{2,1,0:T(4,128)S(1)}, f32[1,3,129]{2,1,0:T(4,128)S(1)}, u32[]{:S(2)}, u32[]{:S(2)}) collective-permute-start(f32[1,3,129]{2,1,0:T(4,128)S(1)} %get-tuple-element.387), channel_id=1, source_target_pairs={{0,8},{8,16},{16,24},{1,9},{9,17},{17,25},{2,10},{10,18},{18,26},{... | collective-permute-start | bytes 4652 | tf_op jit(solution)/shard_map/ppermute | solution.py:23
  12.8 9.5 %collective-permute-start.30 = (f32[1,2,65]{2,1,0:T(2,128)S(1)}, f32[1,2,65]{2,1,0:T(2,128)S(1)}, u32[]{:S(2)}, u32[]{:S(2)}) collective-permute-start(f32[1,2,65]{2,1,0:T(2,128)S(1)} %get-tuple-element.509), channel_id=1, source_target_pairs={{0,8},{8,16},{16,24},{1,9},{9,17},{17,25},{2,10},{10,18},{18,26},{... | collective-permute-start | bytes 1568 | tf_op jit(solution)/shard_map/ppermute | solution.py:23
  16.5 7.2 %collective-permute-start.31 = (f32[1,2,65]{2,1,0:T(2,128)S(1)}, f32[1,2,65]{2,1,0:T(2,128)S(1)}, u32[]{:S(2)}, u32[]{:S(2)}) collective-permute-start(f32[1,2,65]{2,1,0:T(2,128)S(1)} %get-tuple-element.510), channel_id=1, source_target_pairs={{8,0},{16,8},{24,16},{9,1},{17,9},{25,17},{10,2},{18,10},{26,18},{... | collective-permute-start | bytes 1568 | tf_op jit(solution)/shard_map/ppermute | solution.py:25
  22.3 8.5 %collective-permute-start.19 = (f32[1,3,129]{2,1,0:T(4,128)S(1)}, f32[1,3,129]{2,1,0:T(4,128)S(1)}, u32[]{:S(2)}, u32[]{:S(2)}) collective-permute-start(f32[1,3,129]{2,1,0:T(4,128)S(1)} %get-tuple-element.388), channel_id=1, source_target_pairs={{8,0},{16,8},{24,16},{9,1},{17,9},{25,17},{10,2},{18,10},{26,18},{... | collective-permute-start | bytes 4652 | tf_op jit(solution)/shard_map/ppermute | solution.py:25
  23.6 41.8 %collective-permute-start = (f32[1,5,257]{2,1,0:T(8,128)S(1)}, f32[1,5,257]{2,1,0:T(8,128)S(1)}, u32[]{:S(2)}, u32[]{:S(2)}) collective-permute-start(f32[1,5,257]{2,1,0:T(8,128)S(1)} %get-tuple-element.131), channel_id=1, source_target_pairs={{0,8},{8,16},{16,24},{1,9},{9,17},{17,25},{2,10},{10,18},{18,26},{... | collective-permute-start | bytes 15428 | tf_op jit(solution)/shard_map/ppermute | solution.py:23
  27.3 4.8 %collective-permute-start.32 = (f32[4,1,65]{2,1,0:T(1,128)S(1)}, f32[4,1,65]{2,1,0:T(1,128)S(1)}, u32[]{:S(2)}, u32[]{:S(2)}) collective-permute-start(f32[4,1,65]{2,1,0:T(1,128)S(1)} %get-tuple-element.468), channel_id=1, source_target_pairs={{0,2},{2,4},{4,6},{1,3},{3,5},{5,7},{8,10},{10,12},{12,14},{9,11},... | collective-permute-start | bytes 3128 | tf_op jit(solution)/shard_map/ppermute | solution.py:23
  30.8 5.5 %collective-permute-start.33 = (f32[4,1,65]{2,1,0:T(1,128)S(1)}, f32[4,1,65]{2,1,0:T(1,128)S(1)}, u32[]{:S(2)}, u32[]{:S(2)}) collective-permute-start(f32[4,1,65]{2,1,0:T(1,128)S(1)} %get-tuple-element.469), channel_id=1, source_target_pairs={{2,0},{4,2},{6,4},{3,1},{5,3},{7,5},{10,8},{12,10},{14,12},{11,9},... | collective-permute-start | bytes 3128 | tf_op jit(solution)/shard_map/ppermute | solution.py:25
  36.4 4.8 %collective-permute-start.34 = (f32[4,4,1]{2,1,0:T(4,128)S(1)}, f32[4,4,1]{2,1,0:T(4,128)S(1)}, u32[]{:S(2)}, u32[]{:S(2)}) collective-permute-start(f32[4,4,1]{2,1,0:T(4,128)S(1)} %get-tuple-element.411), channel_id=1, source_target_pairs={{0,1},{2,3},{4,5},{6,7},{8,9},{10,11},{12,13},{14,15},{16,17},{18,... | collective-permute-start | bytes 200 | tf_op jit(solution)/shard_map/ppermute | solution.py:23
  39.8 5.5 %collective-permute-start.35 = (f32[4,4,1]{2,1,0:T(4,128)S(1)}, f32[4,4,1]{2,1,0:T(4,128)S(1)}, u32[]{:S(2)}, u32[]{:S(2)}) collective-permute-start(f32[4,4,1]{2,1,0:T(4,128)S(1)} %get-tuple-element.412), channel_id=1, source_target_pairs={{1,0},{3,2},{5,4},{7,6},{9,8},{11,10},{13,12},{15,14},{17,16},{19,... | collective-permute-start | bytes 200 | tf_op jit(solution)/shard_map/ppermute | solution.py:25
  41.2 5.6 %collective-permute-start.20 = (f32[5,1,129]{2,1,0:T(1,128)S(1)}, f32[5,1,129]{2,1,0:T(1,128)S(1)}, u32[]{:S(2)}, u32[]{:S(2)}) collective-permute-start(f32[5,1,129]{2,1,0:T(1,128)S(1)} %get-tuple-element.289), channel_id=1, source_target_pairs={{0,2},{2,4},{4,6},{1,3},{3,5},{5,7},{8,10},{10,12},{12,14},{9,11},... | collective-permute-start | bytes 7748 | tf_op jit(solution)/shard_map/ppermute | solution.py:23
  45.4 5.5 %collective-permute-start.21 = (f32[5,1,129]{2,1,0:T(1,128)S(1)}, f32[5,1,129]{2,1,0:T(1,128)S(1)}, u32[]{:S(2)}, u32[]{:S(2)}) collective-permute-start(f32[5,1,129]{2,1,0:T(1,128)S(1)} %get-tuple-element.290), channel_id=1, source_target_pairs={{2,0},{4,2},{6,4},{3,1},{5,3},{7,5},{10,8},{12,10},{14,12},{11,9},... | collective-permute-start | bytes 7748 | tf_op jit(solution)/shard_map/ppermute | solution.py:25
  50.9 5.3 %collective-permute-start.22 = (f32[5,5,1]{2,1,0:T(8,128)S(1)}, f32[5,5,1]{2,1,0:T(8,128)S(1)}, u32[]{:S(2)}, u32[]{:S(2)}) collective-permute-start(f32[5,5,1]{2,1,0:T(8,128)S(1)} %get-tuple-element.257), channel_id=1, source_target_pairs={{0,1},{2,3},{4,5},{6,7},{8,9},{10,11},{12,13},{14,15},{16,17},{18,... | collective-permute-start | bytes 308 | tf_op jit(solution)/shard_map/ppermute | solution.py:23
  54.7 5.7 %collective-permute-start.23 = (f32[5,5,1]{2,1,0:T(8,128)S(1)}, f32[5,5,1]{2,1,0:T(8,128)S(1)}, u32[]{:S(2)}, u32[]{:S(2)}) collective-permute-start(f32[5,5,1]{2,1,0:T(8,128)S(1)} %get-tuple-element.258), channel_id=1, source_target_pairs={{1,0},{3,2},{5,4},{7,6},{9,8},{11,10},{13,12},{15,14},{17,16},{19,... | collective-permute-start | bytes 308 | tf_op jit(solution)/shard_map/ppermute | solution.py:25
  56.2 9.2 %collective-permute-start.1 = (f32[1,5,257]{2,1,0:T(8,128)S(1)}, f32[1,5,257]{2,1,0:T(8,128)S(1)}, u32[]{:S(2)}, u32[]{:S(2)}) collective-permute-start(f32[1,5,257]{2,1,0:T(8,128)S(1)} %get-tuple-element.132), channel_id=1, source_target_pairs={{8,0},{16,8},{24,16},{9,1},{17,9},{25,17},{10,2},{18,10},{26,18},{... | collective-permute-start | bytes 15428 | tf_op jit(solution)/shard_map/ppermute | solution.py:25
  60.6 10.7 %collective-permute-start.8 = (f32[7,1,257]{2,1,0:T(1,128)S(1)}, f32[7,1,257]{2,1,0:T(1,128)S(1)}, u32[]{:S(2)}, u32[]{:S(2)}) collective-permute-start(f32[7,1,257]{2,1,0:T(1,128)S(1)} %get-tuple-element.143), channel_id=1, source_target_pairs={{0,2},{2,4},{4,6},{1,3},{3,5},{5,7},{8,10},{10,12},{12,14},{9,11},... | collective-permute-start | bytes 21596 | tf_op jit(solution)/shard_map/ppermute | solution.py:23
  64.1 7.2 %collective-permute-start.9 = (f32[7,1,257]{2,1,0:T(1,128)S(1)}, f32[7,1,257]{2,1,0:T(1,128)S(1)}, u32[]{:S(2)}, u32[]{:S(2)}) collective-permute-start(f32[7,1,257]{2,1,0:T(1,128)S(1)} %get-tuple-element.144), channel_id=1, source_target_pairs={{2,0},{4,2},{6,4},{3,1},{5,3},{7,5},{10,8},{12,10},{14,12},{11,9},... | collective-permute-start | bytes 21596 | tf_op jit(solution)/shard_map/ppermute | solution.py:25
  65.5 8.9 %collective-permute-start.2 = (f32[7,1,257]{2,1,0:T(1,128)S(1)}, f32[7,1,257]{2,1,0:T(1,128)S(1)}, u32[]{:S(2)}, u32[]{:S(2)}) collective-permute-start(f32[7,1,257]{2,1,0:T(1,128)S(1)} %get-tuple-element.141), channel_id=1, source_target_pairs={{0,2},{2,4},{4,6},{1,3},{3,5},{5,7},{8,10},{10,12},{12,14},{9,11},... | collective-permute-start | bytes 21596 | tf_op jit(solution)/shard_map/ppermute | solution.py:23
  70.0 5.6 %collective-permute-start.3 = (f32[7,1,257]{2,1,0:T(1,128)S(1)}, f32[7,1,257]{2,1,0:T(1,128)S(1)}, u32[]{:S(2)}, u32[]{:S(2)}) collective-permute-start(f32[7,1,257]{2,1,0:T(1,128)S(1)} %get-tuple-element.142), channel_id=1, source_target_pairs={{2,0},{4,2},{6,4},{3,1},{5,3},{7,5},{10,8},{12,10},{14,12},{11,9},... | collective-permute-start | bytes 21596 | tf_op jit(solution)/shard_map/ppermute | solution.py:25
  71.4 8.9 %collective-permute-start.10 = (f32[7,7,1]{2,1,0:T(8,128)S(1)}, f32[7,7,1]{2,1,0:T(8,128)S(1)}, u32[]{:S(2)}, u32[]{:S(2)}) collective-permute-start(f32[7,7,1]{2,1,0:T(8,128)S(1)} %get-tuple-element.125), channel_id=1, source_target_pairs={{0,1},{2,3},{4,5},{6,7},{8,9},{10,11},{12,13},{14,15},{16,17},{18,... | collective-permute-start | bytes 596 | tf_op jit(solution)/shard_map/ppermute | solution.py:23
  73.0 7.2 %collective-permute-start.11 = (f32[7,7,1]{2,1,0:T(8,128)S(1)}, f32[7,7,1]{2,1,0:T(8,128)S(1)}, u32[]{:S(2)}, u32[]{:S(2)}) collective-permute-start(f32[7,7,1]{2,1,0:T(8,128)S(1)} %get-tuple-element.126), channel_id=1, source_target_pairs={{1,0},{3,2},{5,4},{7,6},{9,8},{11,10},{13,12},{15,14},{17,16},{19,... | collective-permute-start | bytes 596 | tf_op jit(solution)/shard_map/ppermute | solution.py:25
  75.6 5.0 %collective-permute-start.4 = (f32[7,7,1]{2,1,0:T(8,128)S(1)}, f32[7,7,1]{2,1,0:T(8,128)S(1)}, u32[]{:S(2)}, u32[]{:S(2)}) collective-permute-start(f32[7,7,1]{2,1,0:T(8,128)S(1)} %get-tuple-element.123), channel_id=1, source_target_pairs={{0,1},{2,3},{4,5},{6,7},{8,9},{10,11},{12,13},{14,15},{16,17},{18,... | collective-permute-start | bytes 596 | tf_op jit(solution)/shard_map/ppermute | solution.py:23
  78.9 5.8 %collective-permute-start.5 = (f32[7,7,1]{2,1,0:T(8,128)S(1)}, f32[7,7,1]{2,1,0:T(8,128)S(1)}, u32[]{:S(2)}, u32[]{:S(2)}) collective-permute-start(f32[7,7,1]{2,1,0:T(8,128)S(1)} %get-tuple-element.124), channel_id=1, source_target_pairs={{1,0},{3,2},{5,4},{7,6},{9,8},{11,10},{13,12},{15,14},{17,16},{19,... | collective-permute-start | bytes 596 | tf_op jit(solution)/shard_map/ppermute | solution.py:25
  90.5 5.4 %collective-permute-start.13 = (f32[1,3,129]{2,1,0:T(4,128)S(1)}, f32[1,3,129]{2,1,0:T(4,128)S(1)}, u32[]{:S(2)}, u32[]{:S(2)}) collective-permute-start(f32[1,3,129]{2,1,0:T(4,128)S(1)} %get-tuple-element.392), channel_id=1, source_target_pairs={{8,0},{16,8},{24,16},{9,1},{17,9},{25,17},{10,2},{18,10},{26,18},{... | collective-permute-start | bytes 4652 | tf_op jit(solution)/shard_map/ppermute | solution.py:25
  95.9 5.9 %collective-permute-start.14 = (f32[5,1,129]{2,1,0:T(1,128)S(1)}, f32[5,1,129]{2,1,0:T(1,128)S(1)}, u32[]{:S(2)}, u32[]{:S(2)}) collective-permute-start(f32[5,1,129]{2,1,0:T(1,128)S(1)} %get-tuple-element.291), channel_id=1, source_target_pairs={{0,2},{2,4},{4,6},{1,3},{3,5},{5,7},{8,10},{10,12},{12,14},{9,11},... | collective-permute-start | bytes 7748 | tf_op jit(solution)/shard_map/ppermute | solution.py:23
  100.5 5.5 %collective-permute-start.15 = (f32[5,1,129]{2,1,0:T(1,128)S(1)}, f32[5,1,129]{2,1,0:T(1,128)S(1)}, u32[]{:S(2)}, u32[]{:S(2)}) collective-permute-start(f32[5,1,129]{2,1,0:T(1,128)S(1)} %get-tuple-element.292), channel_id=1, source_target_pairs={{2,0},{4,2},{6,4},{3,1},{5,3},{7,5},{10,8},{12,10},{14,12},{11,9},... | collective-permute-start | bytes 7748 | tf_op jit(solution)/shard_map/ppermute | solution.py:25
  107.6 5.7 %collective-permute-start.17 = (f32[5,5,1]{2,1,0:T(8,128)S(1)}, f32[5,5,1]{2,1,0:T(8,128)S(1)}, u32[]{:S(2)}, u32[]{:S(2)}) collective-permute-start(f32[5,5,1]{2,1,0:T(8,128)S(1)} %get-tuple-element.263), channel_id=1, source_target_pairs={{1,0},{3,2},{5,4},{7,6},{9,8},{11,10},{13,12},{15,14},{17,16},{19,... | collective-permute-start | bytes 308 | tf_op jit(solution)/shard_map/ppermute | solution.py:25
  116.0 5.5 %collective-permute-start.25 = (f32[1,2,65]{2,1,0:T(2,128)S(1)}, f32[1,2,65]{2,1,0:T(2,128)S(1)}, u32[]{:S(2)}, u32[]{:S(2)}) collective-permute-start(f32[1,2,65]{2,1,0:T(2,128)S(1)} %get-tuple-element.517), channel_id=1, source_target_pairs={{8,0},{16,8},{24,16},{9,1},{17,9},{25,17},{10,2},{18,10},{26,18},{... | collective-permute-start | bytes 1568 | tf_op jit(solution)/shard_map/ppermute | solution.py:25
  123.4 5.5 %collective-permute-start.27 = (f32[4,1,65]{2,1,0:T(1,128)S(1)}, f32[4,1,65]{2,1,0:T(1,128)S(1)}, u32[]{:S(2)}, u32[]{:S(2)}) collective-permute-start(f32[4,1,65]{2,1,0:T(1,128)S(1)} %get-tuple-element.473), channel_id=1, source_target_pairs={{2,0},{4,2},{6,4},{3,1},{5,3},{7,5},{10,8},{12,10},{14,12},{11,9},... | collective-permute-start | bytes 3128 | tf_op jit(solution)/shard_map/ppermute | solution.py:25
  130.6 5.5 %collective-permute-start.29 = (f32[4,4,1]{2,1,0:T(4,128)S(1)}, f32[4,4,1]{2,1,0:T(4,128)S(1)}, u32[]{:S(2)}, u32[]{:S(2)}) collective-permute-start(f32[4,4,1]{2,1,0:T(4,128)S(1)} %get-tuple-element.416), channel_id=1, source_target_pairs={{1,0},{3,2},{5,4},{7,6},{9,8},{11,10},{13,12},{15,14},{17,16},{19,... | collective-permute-start | bytes 200 | tf_op jit(solution)/shard_map/ppermute | solution.py:25
  138.2 5.5 %collective-permute-start.37 = (f32[1,2,65]{2,1,0:T(2,128)S(1)}, f32[1,2,65]{2,1,0:T(2,128)S(1)}, u32[]{:S(2)}, u32[]{:S(2)}) collective-permute-start(f32[1,2,65]{2,1,0:T(2,128)S(1)} %get-tuple-element.501), channel_id=1, source_target_pairs={{8,0},{16,8},{24,16},{9,1},{17,9},{25,17},{10,2},{18,10},{26,18},{... | collective-permute-start | bytes 1568 | tf_op jit(solution)/shard_map/ppermute | solution.py:25
  145.6 5.5 %collective-permute-start.39 = (f32[4,1,65]{2,1,0:T(1,128)S(1)}, f32[4,1,65]{2,1,0:T(1,128)S(1)}, u32[]{:S(2)}, u32[]{:S(2)}) collective-permute-start(f32[4,1,65]{2,1,0:T(1,128)S(1)} %get-tuple-element.450), channel_id=1, source_target_pairs={{2,0},{4,2},{6,4},{3,1},{5,3},{7,5},{10,8},{12,10},{14,12},{11,9},... | collective-permute-start | bytes 3128 | tf_op jit(solution)/shard_map/ppermute | solution.py:25
  152.9 5.5 %collective-permute-start.41 = (f32[4,4,1]{2,1,0:T(4,128)S(1)}, f32[4,4,1]{2,1,0:T(4,128)S(1)}, u32[]{:S(2)}, u32[]{:S(2)}) collective-permute-start(f32[4,4,1]{2,1,0:T(4,128)S(1)} %get-tuple-element.408), channel_id=1, source_target_pairs={{1,0},{3,2},{5,4},{7,6},{9,8},{11,10},{13,12},{15,14},{17,16},{19,... | collective-permute-start | bytes 200 | tf_op jit(solution)/shard_map/ppermute | solution.py:25
  161.2 5.5 %collective-permute-start.43 = (f32[1,3,129]{2,1,0:T(4,128)S(1)}, f32[1,3,129]{2,1,0:T(4,128)S(1)}, u32[]{:S(2)}, u32[]{:S(2)}) collective-permute-start(f32[1,3,129]{2,1,0:T(4,128)S(1)} %get-tuple-element.362), channel_id=1, source_target_pairs={{8,0},{16,8},{24,16},{9,1},{17,9},{25,17},{10,2},{18,10},{26,18},{... | collective-permute-start | bytes 4652 | tf_op jit(solution)/shard_map/ppermute | solution.py:25
  168.6 5.5 %collective-permute-start.45 = (f32[5,1,129]{2,1,0:T(1,128)S(1)}, f32[5,1,129]{2,1,0:T(1,128)S(1)}, u32[]{:S(2)}, u32[]{:S(2)}) collective-permute-start(f32[5,1,129]{2,1,0:T(1,128)S(1)} %get-tuple-element.288), channel_id=1, source_target_pairs={{2,0},{4,2},{6,4},{3,1},{5,3},{7,5},{10,8},{12,10},{14,12},{11,9},... | collective-permute-start | bytes 7748 | tf_op jit(solution)/shard_map/ppermute | solution.py:25
  175.8 5.7 %collective-permute-start.47 = (f32[5,5,1]{2,1,0:T(8,128)S(1)}, f32[5,5,1]{2,1,0:T(8,128)S(1)}, u32[]{:S(2)}, u32[]{:S(2)}) collective-permute-start(f32[5,5,1]{2,1,0:T(8,128)S(1)} %get-tuple-element.253), channel_id=1, source_target_pairs={{1,0},{3,2},{5,4},{7,6},{9,8},{11,10},{13,12},{15,14},{17,16},{19,... | collective-permute-start | bytes 308 | tf_op jit(solution)/shard_map/ppermute | solution.py:25
  187.2 5.7 %collective-permute-start.49 = (f32[1,5,257]{2,1,0:T(8,128)S(1)}, f32[1,5,257]{2,1,0:T(8,128)S(1)}, u32[]{:S(2)}, u32[]{:S(2)}) collective-permute-start(f32[1,5,257]{2,1,0:T(8,128)S(1)} %get-tuple-element.218), channel_id=1, source_target_pairs={{8,0},{16,8},{24,16},{9,1},{17,9},{25,17},{10,2},{18,10},{26,18},{... | collective-permute-start | bytes 15428 | tf_op jit(solution)/shard_map/ppermute | solution.py:25
  194.8 5.6 %collective-permute-start.51 = (f32[7,1,257]{2,1,0:T(1,128)S(1)}, f32[7,1,257]{2,1,0:T(1,128)S(1)}, u32[]{:S(2)}, u32[]{:S(2)}) collective-permute-start(f32[7,1,257]{2,1,0:T(1,128)S(1)} %get-tuple-element.140), channel_id=1, source_target_pairs={{2,0},{4,2},{6,4},{3,1},{5,3},{7,5},{10,8},{12,10},{14,12},{11,9},... | collective-permute-start | bytes 21596 | tf_op jit(solution)/shard_map/ppermute | solution.py:25
  202.1 5.8 %collective-permute-start.53 = (f32[7,7,1]{2,1,0:T(8,128)S(1)}, f32[7,7,1]{2,1,0:T(8,128)S(1)}, u32[]{:S(2)}, u32[]{:S(2)}) collective-permute-start(f32[7,7,1]{2,1,0:T(8,128)S(1)} %get-tuple-element.122), channel_id=1, source_target_pairs={{1,0},{3,2},{5,4},{7,6},{9,8},{11,10},{13,12},{15,14},{17,16},{19,... | collective-permute-start | bytes 596 | tf_op jit(solution)/shard_map/ppermute | solution.py:25
  218.1 5.1 %collective-permute-start.55 = (f32[1,5,257]{2,1,0:T(8,128)S(1)}, f32[1,5,257]{2,1,0:T(8,128)S(1)}, u32[]{:S(2)}, u32[]{:S(2)}) collective-permute-start(f32[1,5,257]{2,1,0:T(8,128)S(1)} %get-tuple-element.130), channel_id=1, source_target_pairs={{8,0},{16,8},{24,16},{9,1},{17,9},{25,17},{10,2},{18,10},{26,18},{... | collective-permute-start | bytes 15428 | tf_op jit(solution)/shard_map/ppermute | solution.py:25
  225.1 5.6 %collective-permute-start.57 = (f32[7,1,257]{2,1,0:T(1,128)S(1)}, f32[7,1,257]{2,1,0:T(1,128)S(1)}, u32[]{:S(2)}, u32[]{:S(2)}) collective-permute-start(f32[7,1,257]{2,1,0:T(1,128)S(1)} %get-tuple-element.138), channel_id=1, source_target_pairs={{2,0},{4,2},{6,4},{3,1},{5,3},{7,5},{10,8},{12,10},{14,12},{11,9},... | collective-permute-start | bytes 21596 | tf_op jit(solution)/shard_map/ppermute | solution.py:25
  232.4 5.8 %collective-permute-start.59 = (f32[7,7,1]{2,1,0:T(8,128)S(1)}, f32[7,7,1]{2,1,0:T(8,128)S(1)}, u32[]{:S(2)}, u32[]{:S(2)}) collective-permute-start(f32[7,7,1]{2,1,0:T(8,128)S(1)} %get-tuple-element.120), channel_id=1, source_target_pairs={{1,0},{3,2},{5,4},{7,6},{9,8},{11,10},{13,12},{15,14},{17,16},{19,... | collective-permute-start | bytes 596 | tf_op jit(solution)/shard_map/ppermute | solution.py:25
  282.4 5.6 %collective-permute-start.61 = (f32[1,3,129]{2,1,0:T(4,128)S(1)}, f32[1,3,129]{2,1,0:T(4,128)S(1)}, u32[]{:S(2)}, u32[]{:S(2)}) collective-permute-start(f32[1,3,129]{2,1,0:T(4,128)S(1)} %get-tuple-element.356), channel_id=1, source_target_pairs={{8,0},{16,8},{24,16},{9,1},{17,9},{25,17},{10,2},{18,10},{26,18},{... | collective-permute-start | bytes 4652 | tf_op jit(solution)/shard_map/ppermute | solution.py:25
  288.0 5.2 %collective-permute-start.62 = (f32[5,1,129]{2,1,0:T(1,128)S(1)}, f32[5,1,129]{2,1,0:T(1,128)S(1)}, u32[]{:S(2)}, u32[]{:S(2)}) collective-permute-start(f32[5,1,129]{2,1,0:T(1,128)S(1)} %get-tuple-element.283), channel_id=1, source_target_pairs={{0,2},{2,4},{4,6},{1,3},{3,5},{5,7},{8,10},{10,12},{12,14},{9,11},... | collective-permute-start | bytes 7748 | tf_op jit(solution)/shard_map/ppermute | solution.py:23
  291.9 5.5 %collective-permute-start.63 = (f32[5,1,129]{2,1,0:T(1,128)S(1)}, f32[5,1,129]{2,1,0:T(1,128)S(1)}, u32[]{:S(2)}, u32[]{:S(2)}) collective-permute-start(f32[5,1,129]{2,1,0:T(1,128)S(1)} %get-tuple-element.284), channel_id=1, source_target_pairs={{2,0},{4,2},{6,4},{3,1},{5,3},{7,5},{10,8},{12,10},{14,12},{11,9},... | collective-permute-start | bytes 7748 | tf_op jit(solution)/shard_map/ppermute | solution.py:25
  297.4 5.6 %collective-permute-start.64 = (f32[5,5,1]{2,1,0:T(8,128)S(1)}, f32[5,5,1]{2,1,0:T(8,128)S(1)}, u32[]{:S(2)}, u32[]{:S(2)}) collective-permute-start(f32[5,5,1]{2,1,0:T(8,128)S(1)} %get-tuple-element.245), channel_id=1, source_target_pairs={{0,1},{2,3},{4,5},{6,7},{8,9},{10,11},{12,13},{14,15},{16,17},{18,... | collective-permute-start | bytes 308 | tf_op jit(solution)/shard_map/ppermute | solution.py:23
  301.5 5.7 %collective-permute-start.65 = (f32[5,5,1]{2,1,0:T(8,128)S(1)}, f32[5,5,1]{2,1,0:T(8,128)S(1)}, u32[]{:S(2)}, u32[]{:S(2)}) collective-permute-start(f32[5,5,1]{2,1,0:T(8,128)S(1)} %get-tuple-element.246), channel_id=1, source_target_pairs={{1,0},{3,2},{5,4},{7,6},{9,8},{11,10},{13,12},{15,14},{17,16},{19,... | collective-permute-start | bytes 308 | tf_op jit(solution)/shard_map/ppermute | solution.py:25
  309.9 5.5 %collective-permute-start.67 = (f32[1,2,65]{2,1,0:T(2,128)S(1)}, f32[1,2,65]{2,1,0:T(2,128)S(1)}, u32[]{:S(2)}, u32[]{:S(2)}) collective-permute-start(f32[1,2,65]{2,1,0:T(2,128)S(1)} %get-tuple-element.494), channel_id=1, source_target_pairs={{8,0},{16,8},{24,16},{9,1},{17,9},{25,17},{10,2},{18,10},{26,18},{... | collective-permute-start | bytes 1568 | tf_op jit(solution)/shard_map/ppermute | solution.py:25
  315.3 3.9 collective-permute-start.68
  317.9 5.5 %collective-permute-start.69 = (f32[4,1,65]{2,1,0:T(1,128)S(1)}, f32[4,1,65]{2,1,0:T(1,128)S(1)}, u32[]{:S(2)}, u32[]{:S(2)}) collective-permute-start(f32[4,1,65]{2,1,0:T(1,128)S(1)} %get-tuple-element.446), channel_id=1, source_target_pairs={{2,0},{4,2},{6,4},{3,1},{5,3},{7,5},{10,8},{12,10},{14,12},{11,9},... | collective-permute-start | bytes 3128 | tf_op jit(solution)/shard_map/ppermute | solution.py:25
  325.1 5.5 %collective-permute-start.71 = (f32[4,4,1]{2,1,0:T(4,128)S(1)}, f32[4,4,1]{2,1,0:T(4,128)S(1)}, u32[]{:S(2)}, u32[]{:S(2)}) collective-permute-start(f32[4,4,1]{2,1,0:T(4,128)S(1)} %get-tuple-element.404), channel_id=1, source_target_pairs={{1,0},{3,2},{5,4},{7,6},{9,8},{11,10},{13,12},{15,14},{17,16},{19,... | collective-permute-start | bytes 200 | tf_op jit(solution)/shard_map/ppermute | solution.py:25
  332.8 5.5 %collective-permute-start.73 = (f32[1,2,65]{2,1,0:T(2,128)S(1)}, f32[1,2,65]{2,1,0:T(2,128)S(1)}, u32[]{:S(2)}, u32[]{:S(2)}) collective-permute-start(f32[1,2,65]{2,1,0:T(2,128)S(1)} %get-tuple-element.486), channel_id=1, source_target_pairs={{8,0},{16,8},{24,16},{9,1},{17,9},{25,17},{10,2},{18,10},{26,18},{... | collective-permute-start | bytes 1568 | tf_op jit(solution)/shard_map/ppermute | solution.py:25
  340.2 5.5 %collective-permute-start.75 = (f32[4,1,65]{2,1,0:T(1,128)S(1)}, f32[4,1,65]{2,1,0:T(1,128)S(1)}, u32[]{:S(2)}, u32[]{:S(2)}) collective-permute-start(f32[4,1,65]{2,1,0:T(1,128)S(1)} %get-tuple-element.428), channel_id=1, source_target_pairs={{2,0},{4,2},{6,4},{3,1},{5,3},{7,5},{10,8},{12,10},{14,12},{11,9},... | collective-permute-start | bytes 3128 | tf_op jit(solution)/shard_map/ppermute | solution.py:25
  347.4 5.5 %collective-permute-start.77 = (f32[4,4,1]{2,1,0:T(4,128)S(1)}, f32[4,4,1]{2,1,0:T(4,128)S(1)}, u32[]{:S(2)}, u32[]{:S(2)}) collective-permute-start(f32[4,4,1]{2,1,0:T(4,128)S(1)} %get-tuple-element.400), channel_id=1, source_target_pairs={{1,0},{3,2},{5,4},{7,6},{9,8},{11,10},{13,12},{15,14},{17,16},{19,... | collective-permute-start | bytes 200 | tf_op jit(solution)/shard_map/ppermute | solution.py:25
  355.7 5.5 %collective-permute-start.79 = (f32[1,3,129]{2,1,0:T(4,128)S(1)}, f32[1,3,129]{2,1,0:T(4,128)S(1)}, u32[]{:S(2)}, u32[]{:S(2)}) collective-permute-start(f32[1,3,129]{2,1,0:T(4,128)S(1)} %get-tuple-element.330), channel_id=1, source_target_pairs={{8,0},{16,8},{24,16},{9,1},{17,9},{25,17},{10,2},{18,10},{26,18},{... | collective-permute-start | bytes 4652 | tf_op jit(solution)/shard_map/ppermute | solution.py:25
  363.1 5.5 %collective-permute-start.81 = (f32[5,1,129]{2,1,0:T(1,128)S(1)}, f32[5,1,129]{2,1,0:T(1,128)S(1)}, u32[]{:S(2)}, u32[]{:S(2)}) collective-permute-start(f32[5,1,129]{2,1,0:T(1,128)S(1)} %get-tuple-element.282), channel_id=1, source_target_pairs={{2,0},{4,2},{6,4},{3,1},{5,3},{7,5},{10,8},{12,10},{14,12},{11,9},... | collective-permute-start | bytes 7748 | tf_op jit(solution)/shard_map/ppermute | solution.py:25
  370.3 5.7 %collective-permute-start.83 = (f32[5,5,1]{2,1,0:T(8,128)S(1)}, f32[5,5,1]{2,1,0:T(8,128)S(1)}, u32[]{:S(2)}, u32[]{:S(2)}) collective-permute-start(f32[5,5,1]{2,1,0:T(8,128)S(1)} %get-tuple-element.241), channel_id=1, source_target_pairs={{1,0},{3,2},{5,4},{7,6},{9,8},{11,10},{13,12},{15,14},{17,16},{19,... | collective-permute-start | bytes 308 | tf_op jit(solution)/shard_map/ppermute | solution.py:25
  380.6 5.5 %collective-permute-start.85 = (f32[1,5,257]{2,1,0:T(8,128)S(1)}, f32[1,5,257]{2,1,0:T(8,128)S(1)}, u32[]{:S(2)}, u32[]{:S(2)}) collective-permute-start(f32[1,5,257]{2,1,0:T(8,128)S(1)} %get-tuple-element.202), channel_id=1, source_target_pairs={{8,0},{16,8},{24,16},{9,1},{17,9},{25,17},{10,2},{18,10},{26,18},{... | collective-permute-start | bytes 15428 | tf_op jit(solution)/shard_map/ppermute | solution.py:25
  388.0 5.6 %collective-permute-start.87 = (f32[7,1,257]{2,1,0:T(1,128)S(1)}, f32[7,1,257]{2,1,0:T(1,128)S(1)}, u32[]{:S(2)}, u32[]{:S(2)}) collective-permute-start(f32[7,1,257]{2,1,0:T(1,128)S(1)} %get-tuple-element.136), channel_id=1, source_target_pairs={{2,0},{4,2},{6,4},{3,1},{5,3},{7,5},{10,8},{12,10},{14,12},{11,9},... | collective-permute-start | bytes 21596 | tf_op jit(solution)/shard_map/ppermute | solution.py:25
  395.3 5.8 %collective-permute-start.89 = (f32[7,7,1]{2,1,0:T(8,128)S(1)}, f32[7,7,1]{2,1,0:T(8,128)S(1)}, u32[]{:S(2)}, u32[]{:S(2)}) collective-permute-start(f32[7,7,1]{2,1,0:T(8,128)S(1)} %get-tuple-element.118), channel_id=1, source_target_pairs={{1,0},{3,2},{5,4},{7,6},{9,8},{11,10},{13,12},{15,14},{17,16},{19,... | collective-permute-start | bytes 596 | tf_op jit(solution)/shard_map/ppermute | solution.py:25
  410.6 5.1 %collective-permute-start.91 = (f32[1,5,257]{2,1,0:T(8,128)S(1)}, f32[1,5,257]{2,1,0:T(8,128)S(1)}, u32[]{:S(2)}, u32[]{:S(2)}) collective-permute-start(f32[1,5,257]{2,1,0:T(8,128)S(1)} %get-tuple-element.128), channel_id=1, source_target_pairs={{8,0},{16,8},{24,16},{9,1},{17,9},{25,17},{10,2},{18,10},{26,18},{... | collective-permute-start | bytes 15428 | tf_op jit(solution)/shard_map/ppermute | solution.py:25
  417.7 5.6 %collective-permute-start.93 = (f32[7,1,257]{2,1,0:T(1,128)S(1)}, f32[7,1,257]{2,1,0:T(1,128)S(1)}, u32[]{:S(2)}, u32[]{:S(2)}) collective-permute-start(f32[7,1,257]{2,1,0:T(1,128)S(1)} %get-tuple-element.134), channel_id=1, source_target_pairs={{2,0},{4,2},{6,4},{3,1},{5,3},{7,5},{10,8},{12,10},{14,12},{11,9},... | collective-permute-start | bytes 21596 | tf_op jit(solution)/shard_map/ppermute | solution.py:25
  424.9 5.8 %collective-permute-start.95 = (f32[7,7,1]{2,1,0:T(8,128)S(1)}, f32[7,7,1]{2,1,0:T(8,128)S(1)}, u32[]{:S(2)}, u32[]{:S(2)}) collective-permute-start(f32[7,7,1]{2,1,0:T(8,128)S(1)} %get-tuple-element.116), channel_id=1, source_target_pairs={{1,0},{3,2},{5,4},{7,6},{9,8},{11,10},{13,12},{15,14},{17,16},{19,... | collective-permute-start | bytes 596 | tf_op jit(solution)/shard_map/ppermute | solution.py:25
  (53 other events, 117.1 us)
where the time goes:
time: 480 us; the launch traced here: 477 us
  starting transfers between devices  172 us (36%)
  waiting for transfers between devices  169 us (35%)
  blocking collectives  76.6 us (16%)
  local copies, waits for them, and re-layouts  27.5 us (6%)
  other arithmetic  17.6 us (4%)
  between operations  10.6 us (2%)
    ppermute x48, waiting for transfers between devices, extended(): lax.ppermute(head, axis, [((i + 1) % count, i) for i in range(ends)])  167 us
    ppermute x48, starting transfers between devices, extended(): lax.ppermute(tail, axis, [(i, (i + 1) % count) for i in range(ends)])  109 us
    psum x2, blocking collectives, inner_pair(): return lax.psum((local_rho, local_curv), ('gx', 'gy', 'gz'))  76.6 us
    ppermute x48, starting transfers between devices, extended(): lax.ppermute(head, axis, [((i + 1) % count, i) for i in range(ends)])  62.4 us
  transfers between devices with their start and end apart: 96, of which 54 were waited for; matrix products, arithmetic and copies ran while one was open for 1% of the time, Pallas kernels for 0%

commit v1 on v0

--- a/solution.py
+++ b/solution.py
@@ -4,6 +4,8 @@
 import jax.numpy as jnp
 import numpy as np
 from jax import lax
+from jax.experimental import pallas as pl
+from jax.experimental.pallas import tpu as pltpu
 from jax.sharding import PartitionSpec as P
 
 LEVELS = 3
@@ -299,12 +301,479 @@
     return (iterate[1:, 1:, 1:], resid[1:, 1:, 1:])
 
 
+def exact_tables():
+    points = np.array([-1.0, -math.sqrt(3.0 / 7.0), 0.0, math.sqrt(3.0 / 7.0), 1.0])
+    quad_weights = np.array([0.1, 49.0 / 90.0, 32.0 / 45.0, 49.0 / 90.0, 0.1])
+    bary = np.array(
+        [np.prod([points[i] - points[k] for k in range(5) if k != i]) for i in range(5)]
+    )
+    deriv = np.zeros((5, 5))
+    for i in range(5):
+        for j in range(5):
+            if i != j:
+                deriv[i, j] = bary[i] / (bary[j] * (points[i] - points[j]))
+    for i in range(5):
+        deriv[i, i] = -np.sum(deriv[i])
+    return points, quad_weights, deriv
+
+
+def level_widths():
+    points = exact_tables()[0]
+    widths = [[float(h) for h in points[1:] - points[:-1]]]
+    for _ in range(LEVELS - 1):
+        last = widths[-1]
+        widths.append([last[2 * i] + last[2 * i + 1] for i in range(len(last) // 2)])
+    return widths
+
+
+def cell_scales(hx, hy, hz):
+    mass = lambda h, odd: h / 12.0 if odd else h / 4.0
+    scales = {}
+    for p in range(2):
+        for q in range(2):
+            for r in range(2):
+                scale = 0.0
+                if p:
+                    scale += mass(hy, q) * mass(hz, r) / hx
+                if q:
+                    scale += mass(hx, p) * mass(hz, r) / hy
+                if r:
+                    scale += mass(hx, p) * mass(hy, q) / hz
+                scales[p, q, r] = scale
+    return scales
+
+
+def iteration_kernel(place, gathered, x_out, r_out, weighted, full, part, c0, c1, c2,
+                     d0, d1, d2, f1, f2, g1, p1, g2, p2, guess1, resid, precond, direction,
+                     iterate, *, ny):
+    rows, lanes = resid.shape[1:]
+    blocks = 2 * rows
+    stride = gathered.shape[0] // rows
+    half = stride // 2
+    points, quad, deriv = exact_tables()
+    widths = level_widths()
+    cells = [len(h) for h in widths]
+    coeffs, diags = (c0, c1, c2), (d0, d1, d2)
+    fulls, parts = (full, g1, g2), (part, p1, p2)
+
+    sub = lax.broadcasted_iota(jnp.int32, (rows, lanes), 0)
+    lane = lax.broadcasted_iota(jnp.int32, (rows, lanes), 1)
+    masks = (
+        (sub < rows - ny).astype(jnp.float32),
+        (sub % ny < ny - 1).astype(jnp.float32),
+        (lane < lanes - 1).astype(jnp.float32),
+    )
+
+    def before(tile, dim):
+        if dim == 2:
+            return pltpu.roll(tile, 1, 1)
+        return pltpu.roll(tile, (ny, 1)[dim], 0)
+
+    def after(tile, dim):
+        if dim == 2:
+            return pltpu.roll(tile, lanes - 1, 1)
+        return pltpu.roll(tile, rows - (ny, 1)[dim], 0)
+
+    def at(n, a, b, c):
+        return (a * (n + 1) + b) * (n + 1) + c
+
+    def own(n, a, b, c):
+        return ((a - 1) * n + b - 1) * n + c - 1
+
+    def inside(n, a, b, c, tile):
+        for dim, offset in enumerate((a, b, c)):
+            if offset == n:
+                tile = tile * masks[dim]
+        return tile
+
+    def ghosts(ref, n):
+        for a in range(1, n + 1):
+            for b in range(1, n + 1):
+                ref[at(n, a, b, 0)] = before(ref[at(n, a, b, n)], 2)
+            for c in range(n + 1):
+                ref[at(n, a, 0, c)] = before(ref[at(n, a, n, c)], 1)
+        for b in range(n + 1):
+            for c in range(n + 1):
+                ref[at(n, 0, b, c)] = before(ref[at(n, n, b, c)], 0)
+
+    def fold(ref, n):
+        for a in range(n + 1):
+            for b in range(n + 1):
+                ref[at(n, a, b, n)] += after(ref[at(n, a, b, 0)], 2)
+            for c in range(1, n + 1):
+                ref[at(n, a, n, c)] += after(ref[at(n, a, 0, c)], 1)
+        for b in range(1, n + 1):
+            for c in range(1, n + 1):
+                ref[at(n, n, b, c)] += after(ref[at(n, 0, b, c)], 0)
+
+    def owned(n):
+        for a in range(1, n + 1):
+            for b in range(1, n + 1):
+                for c in range(1, n + 1):
+                    yield a, b, c
+
+    def lor(level):
+        n, h = cells[level], widths[level]
+        src, dst, coeff = fulls[level], parts[level], coeffs[level]
+        ghosts(src, n)
+        for b in range(n):
+            for c in range(n):
+                carried = None
+                face = None
+                for a in range(n + 1):
+                    u = [[src[at(n, a, b + i, c + k)] for k in range(2)] for i in range(2)]
+                    sums = [u[i][1] + u[i][0] for i in range(2)]
+                    difs = [u[i][1] - u[i][0] for i in range(2)]
+                    now = {
+                        (0, 0): sums[1] + sums[0],
+                        (1, 0): sums[1] - sums[0],
+                        (0, 1): difs[1] + difs[0],
+                        (1, 1): difs[1] - difs[0],
+                    }
+                    lower = {}
+                    upper = {}
+                    if a > 0:
+                        scales = cell_scales(h[a - 1], h[b], h[c])
+                        k = coeff[own(n, a, b + 1, c + 1)]
+                        for key in now:
+                            odd = ((now[key] - face[key]) * scales[(1,) + key]) * k
+                            if key == (0, 0):
+                                lower[key], upper[key] = -odd, odd
+                            else:
+                                even = ((now[key] + face[key]) * scales[(0,) + key]) * k
+                                lower[key], upper[key] = even - odd, even + odd
+                        total = {
+                            key: lower[key] if carried is None else lower[key] + carried[key]
+                            for key in now
+                        }
+                        spread(dst, n, a - 1, b, c, total)
+                    face = now
+                    carried = upper if a > 0 else None
+                spread(dst, n, n, b, c, carried)
+        fold(dst, n)
+
+    def spread(dst, n, a, b, c, total):
+        s1 = total[0, 0] + total[1, 0]
+        s0 = total[0, 0] - total[1, 0]
+        d1_ = total[0, 1] + total[1, 1]
+        d0_ = total[0, 1] - total[1, 1]
+        for i, s, d in ((0, s0, d0_), (1, s1, d1_)):
+            for k, value in ((0, s - d), (1, s + d)):
+                spot = at(n, a, b + i, c + k)
+                if (i == 1 or b == 0) and (k == 1 or c == 0):
+                    dst[spot] = value
+                else:
+                    dst[spot] += value
+
+    def diagonal(level):
+        n, h = cells[level], widths[level]
+        dst, coeff = parts[level], coeffs[level]
+        tiles = {}
+        for a in range(n):
+            for b in range(n):
+                for c in range(n):
+                    hx, hy, hz = h[a], h[b], h[c]
+                    scale = hy * hz / (9 * hx) + hx * hz / (9 * hy) + hx * hy / (9 * hz)
+                    tile = coeff[own(n, a + 1, b + 1, c + 1)] * scale
+                    for i in range(2):
+                        for j in range(2):
+                            for k in range(2):
+                                spot = at(n, a + i, b + j, c + k)
+                                first = (i or a == 0) and (j or b == 0) and (k or c == 0)
+                                if first:
+                                    dst[spot] = tile
+                                else:
+                                    dst[spot] += tile
+        fold(dst, n)
+        for a, b, c in owned(n):
+            diags[level][own(n, a, b, c)] = relax_weight / dst[at(n, a, b, c)]
+
+    def pair_weights(level):
+        h = widths[level]
+        spans = [(h[2 * i], h[2 * i + 1]) for i in range(len(h) // 2)]
+        return [q / (p + q) for p, q in spans], [p / (p + q) for p, q in spans]
+
+    def restrict_to(level, defect, target):
+        n = cells[level]
+        m = n // 2
+        left, right = pair_weights(level)
+
+        def line(values, dim):
+            result = []
+            for o in range(1, m + 1):
+                beyond = values[2 * o] if o < m else after(values[0], dim)
+                result.append(
+                    values[2 * o - 1] + right[o - 1] * values[2 * o - 2] + left[o % m] * beyond
+                )
+            return result
+
+        slabs = []
+        for a in range(1, n + 1):
+            lines = [line([defect(a, b, c) for c in range(1, n + 1)], 2) for b in range(1, n + 1)]
+            turned = [line([lines[b][c] for b in range(n)], 1) for c in range(m)]
+            slabs.append(turned)
+        for c in range(m):
+            for b in range(m):
+                out = line([slabs[a][c][b] for a in range(n)], 0)
+                for a in range(m):
+                    target[own(m, a + 1, b + 1, c + 1)] = inside(m, a + 1, b + 1, c + 1, out[a])
+
+    def prolong_from(level, add):
+        n = cells[level]
+        m = n // 2
+        left, right = pair_weights(level)
+        src = fulls[level + 1]
+        ghosts(src, m)
+
+        def line(values):
+            result = []
+            for o in range(1, m + 1):
+                result.append(left[o - 1] * values[o - 1] + right[o - 1] * values[o])
+                result.append(values[o])
+            return result
+
+        slabs = []
+        for a in range(m + 1):
+            lines = [line([src[at(m, a, b, c)] for c in range(m + 1)]) for b in range(m + 1)]
+            slabs.append([line([lines[b][c] for b in range(m + 1)]) for c in range(n)])
+        for c in range(n):
+            for b in range(n):
+                out = line([slabs[a][c][b] for a in range(m + 1)])
+                for a in range(n):
+                    add(a + 1, b + 1, c + 1, out[a])
+
+    def cycle_at(level, forcing, store):
+        n = cells[level]
+        src, dst, diag = fulls[level], parts[level], diags[level]
+        for a, b, c in owned(n):
+            spot = own(n, a, b, c)
+            src[at(n, a, b, c)] = forcing[spot] * diag[spot]
+        lor(level)
+        if level < LEVELS - 1:
+            restrict_to(
+                level,
+                lambda a, b, c: forcing[own(n, a, b, c)] - dst[at(n, a, b, c)],
+                (f1, f2)[level],
+            )
+
+            def leave(a, b, c, tile):
+                fulls[level + 1][at(n // 2, a, b, c)] = tile
+
+            cycle_at(level + 1, (f1, f2)[level], leave)
+
+            def add(a, b, c, tile):
+                src[at(n, a, b, c)] += tile
+
+            prolong_from(level, add)
+            lor(level)
+        for a, b, c in owned(n):
+            spot = own(n, a, b, c)
+            change = inside(n, a, b, c, (forcing[spot] - dst[at(n, a, b, c)]) * diag[spot])
+            store(a, b, c, src[at(n, a, b, c)] + change)
+
+    def derive(u):
+        e = [u[0] + u[4], u[1] + u[3], u[2]]
+        o = [u[0] - u[4], u[1] - u[3]]
+        odd = []
+        even = []
+        for i in range(2):
+            odd.append(sum(
+                e[j] * float((deriv[i, j] + deriv[i, 4 - j]) / 2 if j < 2 else deriv[i, 2])
+                for j in range(3)
+            ))
+        for i in range(3):
+            even.append(sum(o[j] * float((deriv[i, j] - deriv[i, 4 - j]) / 2) for j in range(2)))
+        return [even[0] + odd[0], even[1] + odd[1], even[2], even[1] - odd[1], even[0] - odd[0]]
+
+    def derive_back(g):
+        e = [g[0] + g[4], g[1] + g[3], g[2]]
+        o = [g[0] - g[4], g[1] - g[3]]
+        odd = []
+        even = []
+        for a in range(2):
+            odd.append(sum(
+                e[j] * float((deriv[j, a] + deriv[4 - j, a]) / 2 if j < 2 else deriv[2, a])
+                for j in range(3)
+            ))
+        for a in range(3):
+            even.append(sum(o[j] * float((deriv[j, a] - deriv[4 - j, a]) / 2) for j in range(2)))
+        return [even[0] + odd[0], even[1] + odd[1], even[2], even[1] - odd[1], even[0] - odd[0]]
+
+    def stiffness():
+        ghosts(full, 4)
+
+        def run(spots, first):
+            grad = derive([full[s] for s in spots])
+            back = derive_back([grad[i] * weighted[s] for i, s in enumerate(spots)])
+            for s, value in zip(spots, back):
+                if first:
+                    part[s] = value
+                else:
+                    part[s] += value
+
+        def outer(i, carry):
+            for k in range(5):
+                run([25 * i + 5 * k + t for t in range(5)], True)
+            for k in range(5):
+                run([25 * i + 5 * t + k for t in range(5)], False)
+            return carry
+
+        def along(i, carry):
+            for k in range(5):
+                run([25 * t + 5 * i + k for t in range(5)], False)
+            return carry
+
+        lax.fori_loop(0, 5, outer, 0)
+        lax.fori_loop(0, 5, along, 0)
+        fold(part, 4)
+
+    low = lane < lanes // 2
+    for a in range(5):
+        for b in range(5):
+            for c in range(5):
+                spot = 25 * a + 5 * b + c
+                first = gathered[pl.ds(spot, rows, stride=stride), :]
+                second = gathered[pl.ds(half + spot, rows, stride=stride), :]
+                cube = float(quad[a] * quad[b] * quad[c])
+                full[spot] = jnp.where(low, first, pltpu.roll(second, lanes // 2, 1))
+                part[spot] = jnp.where(low, pltpu.roll(first, lanes // 2, 1), second) * cube
+                weighted[spot] = full[spot] * cube
+    fold(part, 4)
+    for a, b, c in owned(4):
+        resid[own(4, a, b, c)] = inside(4, a, b, c, part[at(4, a, b, c)])
+    for a in range(4):
+        for b in range(4):
+            plane = [
+                (full[at(4, a, b, c)] + full[at(4, a + 1, b, c)])
+                + (full[at(4, a, b + 1, c)] + full[at(4, a + 1, b + 1, c)])
+                for c in range(5)
+            ]
+            for c in range(4):
+                c0[own(4, a + 1, b + 1, c + 1)] = (plane[c] + plane[c + 1]) * 0.125
+    for level in range(LEVELS - 1):
+        m = cells[level + 1]
+        for a, b, c in owned(m):
+            total = None
+            for i in range(2):
+                for j in range(2):
+                    for k in range(2):
+                        tile = coeffs[level][
+                            own(2 * m, 2 * a - i, 2 * b - j, 2 * c - k)
+                        ]
+                        total = tile if total is None else total + tile
+            coeffs[level + 1][own(m, a, b, c)] = total * 0.125
+    for level in range(LEVELS):
+        diagonal(level)
+
+    direction[...] = jnp.zeros_like(direction)
+    iterate[...] = jnp.zeros_like(iterate)
+
+    def settle(a, b, c, tile):
+        precond[own(4, a, b, c)] = tile
+
+    def product(tiles):
+        total = None
+        for tile in tiles:
+            total = tile if total is None else total + tile
+        return jnp.sum(jnp.sum(total, axis=0, keepdims=True), axis=1, keepdims=True)
+
+    def step(number, rho_old):
+        cycle_at(0, resid, settle)
+        rho = product(resid[i] * precond[i] for i in range(64))
+        ratio = jnp.where(number == 0, 0.0, rho / rho_old)
+        for a, b, c in owned(4):
+            spot = own(4, a, b, c)
+            value = precond[spot] + ratio * direction[spot]
+            direction[spot] = value
+            full[at(4, a, b, c)] = value
+        stiffness()
+        curv = None
+        for a, b, c in owned(4):
+            image = inside(4, a, b, c, part[at(4, a, b, c)])
+            precond[own(4, a, b, c)] = image
+            term = direction[own(4, a, b, c)] * image
+            curv = term if curv is None else curv + term
+        alpha = rho / product([curv])
+        for i in range(64):
+            iterate[i] += alpha * direction[i]
+            resid[i] -= alpha * precond[i]
+        return rho
+
+    lax.fori_loop(0, 2, step, jnp.ones((1, 1), jnp.float32))
+
+    row = place[0]
+    start = place[1]
+    width = x_out.shape[1]
+    ez = lax.broadcasted_iota(jnp.int32, (lanes, width), 0)
+    spot_z = lax.broadcasted_iota(jnp.int32, (lanes, width), 1)
+    for out, ref in ((x_out, iterate), (r_out, resid)):
+        total = jnp.zeros((16, width), jnp.float32)
+        for c in range(4):
+            pick = (spot_z == 4 * (ez - start) + c).astype(jnp.float32)
+            lines = jnp.concatenate(
+                [ref[4 * ab + c, pl.ds(row, 1), :] for ab in range(16)], axis=0
+            )
+            total = total + jnp.dot(
+                lines, pick, precision=lax.Precision.HIGHEST,
+                preferred_element_type=jnp.float32,
+            )
+        out[...] = total
+
+
+def whole_body(kappa, source):
+    nx, ny = lax.axis_size("gx"), lax.axis_size("gy")
+    rows, lanes = nx * ny, 2 * kappa.shape[5]
+    packed = jnp.concatenate([kappa.reshape(125, -1), source.reshape(125, -1)], axis=1)
+    packed = jnp.pad(packed, ((0, 3), (0, 0)))
+    gathered = lax.all_gather(packed, ("gx", "gy", "gz"), axis=0, tiled=True)
+    place = jnp.stack([
+        lax.axis_index("gx") * ny + lax.axis_index("gy"),
+        lax.axis_index("gz") * kappa.shape[5],
+    ]).astype(jnp.int32)
+
+    def tiles(count):
+        return pltpu.VMEM((count, rows, lanes), jnp.float32)
+
+    counts = [125, 125, 125, 64, 8, 1, 64, 8, 1, 8, 1, 27, 27, 8, 8, 8, 64, 64, 64, 64]
+    width = 2 * lanes
+    shape = jax.ShapeDtypeStruct((16, width), jnp.float32)
+    vmem = pl.BlockSpec(memory_space=pltpu.VMEM)
+    outs = pl.pallas_call(
+        lambda *refs: iteration_kernel(*refs, ny=ny),
+        out_shape=(shape, shape),
+        in_specs=[pl.BlockSpec(memory_space=pltpu.SMEM), vmem],
+        out_specs=(vmem, vmem),
+        scratch_shapes=[tiles(n) for n in counts],
+        compiler_params=pltpu.CompilerParams(vmem_limit_bytes=40 * 2**20),
+        name="whole_iteration",
+    )(place, gathered)
+    return tuple(o.reshape(4, 4, width) for o in outs)
+
+
+def fits_whole(kappa, mesh):
+    sizes = mesh.shape
+    rows = sizes["gx"] * sizes["gy"]
+    one_column = kappa.shape[3] == sizes["gx"] and kappa.shape[4] == sizes["gy"]
+    lanes = kappa.shape[5]
+    return (
+        one_column
+        and sizes["gz"] == 2
+        and rows % 8 == 0
+        and lanes % 128 == 0
+        and rows * lanes <= 16 * 128
+    )
+
+
 def solution(mesh):
     placed = (P(None, None, None, "gx", "gy", "gz"), P(None, None, None, "gx", "gy", "gz"))
-    return jax.shard_map(
-        body,
-        mesh=mesh,
-        in_specs=placed,
-        out_specs=(P("gx", "gy", "gz"), P("gx", "gy", "gz")),
-        check_vma=False,
-    )
+
+    def run(kappa, source):
+        return jax.shard_map(
+            whole_body if fits_whole(kappa, mesh) else body,
+            mesh=mesh,
+            in_specs=placed,
+            out_specs=(P("gx", "gy", "gz"), P("gx", "gy", "gz")),
+            check_vma=False,
+        )(kappa, source)
+
+    return run

time: 480 us -> 93.2 us (0.19)
  starting transfers between devices: 172 us -> 0.04 us
  waiting for transfers between devices: 169 us -> 60 us
  blocking collectives: 76.6 us -> 0 us
  local copies, waits for them, and re-layouts: 27.5 us -> 2.85 us
  other arithmetic: 17.6 us -> 2.79 us
  Pallas kernels: 0 us -> 13.2 us
    ppermute x96 -> x0, starting transfers between devices: 172 us -> none  [the longest x48 109 us: extended(): lax.ppermute(tail, axis, [(i, (i + 1) % count) for i in range(ends)])]
    ppermute x96 -> x0, waiting for transfers between devices: 169 us -> none  [the longest x48 167 us: extended(): lax.ppermute(head, axis, [((i + 1) % count, i) for i in range(ends)])]
    psum x2 -> x0, blocking collectives: 76.6 us -> none  [inner_pair(): return lax.psum((local_rho, local_curv), ('gx', 'gy', 'gz'))]
    all_gather x0 -> x1, waiting for transfers between devices: none -> 60 us  [whole_body(): gathered = lax.all_gather(packed, ('gx', 'gy', 'gz'), axis=0, tiled=True)]
    pallas_call x0 -> x1, Pallas kernels: none -> 13.2 us  [whole_body(): pl.pallas_call(lambda *refs: iteration_kernel(*refs, ny=ny), out_shape=(s...]
    slice x93 -> x0, local copies, waits for them, and re-layouts: 8.07 us -> none  [the longest x11 1.84 us: prolong_first(): return jnp.concatenate([woven, coarse[-1:]], axis=0)]
    unnamed x38 -> x2, local copies, waits for them, and re-layouts: 8.17 us -> 1.59 us
    reshape x25 -> x4, local copies, waits for them, and re-layouts: 7.29 us -> 1.26 us  [the longest x2 1.24 us: whole_body(): return tuple((o.reshape(4, 4, width) for o in outs))]
  transfers between devices with their start and end apart: 96 -> 1, of which waited for: 54 -> 1; matrix products, arithmetic and copies ran while one was open for 1% -> 0% of each run, Pallas kernels for 0% -> 0%
where the time goes in v1:
time: 93.2 us; the launch traced here: 93 us
  waiting for transfers between devices  60 us (64%)
  between operations  14.1 us (15%)
  Pallas kernels  13.2 us (14%)
  local copies, waits for them, and re-layouts  2.85 us (3%)
  other arithmetic  2.79 us (3%)
    all_gather x1, waiting for transfers between devices, whole_body(): gathered = lax.all_gather(packed, ('gx', 'gy', 'gz'), axis=0, tiled=True)  60 us
    pallas_call x1, Pallas kernels, whole_body(): pl.pallas_call(lambda *refs: iteration_kernel(*refs, ny=ny), out_shape=(s...  13.2 us
    unnamed x2, other arithmetic  2 us
  transfers between devices with their start and end apart: 1, of which 1 were waited for; matrix products, arithmetic and copies ran while one was open for 0% of the time, Pallas kernels for 0%

profile of v1, /device:TPU:0, one launch (start us, length us, event | category | flops | bytes accessed | tf_op | source)
XLA Modules:
  0.0 93.0 jit_solution(4237625575033794763)
XLA Ops:
  7.2 0.0 all-gather.2.cloned.1.call-start
  7.2 1.0 %reduce = f32[5,5,5,64]{3,2,1,0:T(8,128)S(1)} reduce(f32[5,5,5,1,1,64]{5,4,3,2,1,0:T(1,128)} %param.2, f32[]{:T(128)} %constant.22), dimensions={3,4}, to_apply=%param.2.reduce_sub_computation | reduce | bytes 64004 | tf_op args[0]
  8.2 1.0 %reduce.1 = f32[5,5,5,64]{3,2,1,0:T(8,128)S(1)} reduce(f32[5,5,5,1,1,64]{5,4,3,2,1,0:T(1,128)} %param.3, f32[]{:T(128)} %constant.22), dimensions={3,4}, to_apply=%param.3.reduce_sub_computation | reduce | bytes 64004 | tf_op args[1]
  9.3 0.7 select_maximum_fusion
  10.0 0.0 all-gather.2.cloned.1.call-update
  10.0 0.1 pad_add_fusion.refs_0_
  10.1 60.0 %all-gather.2.cloned.1.call-done.refs_1_ = f32[4096,128]{1,0:T(8,128)} async-done(((f32[128,128]{1,0:T(8,128)}), f32[4096,128]{1,0:T(8,128)}) %all-gather.2.cloned.1.call-update) | async-done | bytes 2097168 | tf_op jit(solution)/shard_map/all_gather | solution.py:728
  70.1 0.0 copy-start
  70.1 1.6 %copy-done = f32[4096,128]{1,0:T(8,128)S(1)} copy-done((f32[4096,128]{1,0:T(8,128)S(1)}, f32[4096,128]{1,0:T(8,128)}, u32[]{:S(2)}) %copy-start) | copy-done | bytes 2097176
  71.6 13.2 %whole_iteration.1 = (f32[16,256]{1,0:T(8,128)S(1)}, f32[16,256]{1,0:T(8,128)S(1)}) custom-call(s32[2]{0:T(128)S(1)} %pad_add_fusion.refs_0_, f32[4096,128]{1,0:T(8,128)S(1)} %copy-done), custom_call_target="tpu_custom_call" | custom-call | tf_op jit(solution)/shard_map/whole_iteration/pallas_call | solution.py:741
  84.9 0.6 reshape.18
  85.5 0.6 reshape.19
  (2 shorter events, 0.0 us)
Async XLA Ops:
  7.2 62.9 %all-gather.2.cloned.1.call-start = ((), (), s32[]{:S(2)}) async-start(), calls=%async_computation | async-start | bytes 2162688 | tf_op jit(solution)/shard_map/all_gather | solution.py:728
  70.1 1.6 %copy-start = (f32[4096,128]{1,0:T(8,128)S(1)}, f32[4096,128]{1,0:T(8,128)}, u32[]{:S(2)}) copy-start(f32[4096,128]{1,0:T(8,128)} %all-gather.2.cloned.1.call-done.refs_1_) | copy-start | bytes 6291460
Sparse Core Ops, SparseCore 0:
  10.9 59.0 all-gather.1
